TPU v7x, 32 devices: a whole 2x2x4 slice. The times are simulated.
32 devices in a mesh: gx: 8 (over z, y), gy: 4 (over x, core).
Axes of the slice: x: 2, y: 2, z: 4, core: 2. Of those that a mesh axis runs over, the one named last changes fastest.
Arguments:
- anomalies: float32 [80, 16, 32, 128], P(None, 'gx', 'gy'), may hold values from -6 to 6
- state_mean: float32 [16, 32, 128], P('gx', 'gy'), may hold values from -6 to 6
- obs_value: float32 [16, 256], P(None, 'gy'), may hold values from -8 to 8
- obs_cell: int32 [16, 256], replicated, may hold values from 0 to 2047
- owner: int32 [16], replicated, may hold values from 0 to 7, as said below
- order: int32 [16], replicated, may hold values from 0 to 15, each once
- root_inv: float32 [16, 256, 256], P(None, 'gy'), as said below
- gain_inv: float32 [16, 256, 256], P(None, 'gy'), as said below
Outputs:
- post_anomalies: float32 [80, 16, 32, 128], P(None, 'gx', 'gy')
- post_mean: float32 [16, 32, 128], P('gx', 'gy')
Inputs may be any that keep to these rules, and one draw needn't show every extreme that they name: `owner`: some batch lies at slab 8 - 2, some at slab 1 and some at slab 8 // 2; the others favour low slabs. `order`: each batch number once. `root_inv`: symmetric. `gain_inv`: symmetric.
All inputs are finite; a program needn't handle non-finite values.
Results may differ from a plain program's by a relative error of at most 0.0001.
Values sent between devices are 32-bit elements; how exact they have to be, the bound alone decides.
A program may use at most 64 MiB of HBM per device.

v0:
```python
import functools

import jax
import jax.numpy as jnp
from jax import lax
from jax.experimental import pallas as pl
from jax.experimental.pallas import tpu as pltpu
from jax.sharding import PartitionSpec as P

REACH = 3
LANES = 128
MESH = pl.DeviceIdType.MESH
VMEM = pl.BlockSpec(memory_space=pltpu.VMEM)
SMEM = pl.BlockSpec(memory_space=pltpu.SMEM)
F32 = jnp.float32
BF16 = jnp.bfloat16


def split(value):
    high = value.astype(BF16)
    return high, (value - high.astype(F32)).astype(BF16)


def nn(left, right):
    return lax.dot_general(left, right, (((1,), (0,)), ((), ())), preferred_element_type=F32)


def nt(left, right):
    return lax.dot_general(left, right, (((1,), (1,)), ((), ())), preferred_element_type=F32)


def lane_ids(shape):
    return lax.broadcasted_iota(jnp.int32, shape, len(shape) - 1)


def pick_kernel(lon_dev, lat_dev, cells_ref, value_ref, owner_ref, order_ref, anom_ref, mean_ref, state_ref, packed_ref, rows_ref):
    column, band = lax.axis_index("gx"), lax.axis_index("gy")
    members, classes, levels = anom_ref.shape
    batches, quarter = value_ref.shape

    for c in range(classes):
        lat = (band * lat_dev + c % lat_dev).astype(F32)
        lon = (column * lon_dev + c // lat_dev).astype(F32)
        tall = jnp.concatenate(
            [
                anom_ref[:, c, :],
                mean_ref[pl.ds(c, 1), :],
                jnp.full((1, levels), lat, F32),
                jnp.full((1, levels), lon, F32),
                jnp.zeros((LANES - members - 3, levels), F32),
            ],
            axis=0,
        )
        state_ref[pl.ds(c * levels, levels), :] = tall.T

    lane = lane_ids((1, LANES))

    def batch(t, _):
        b = order_ref[t]
        mine = owner_ref[b] == column

        @pl.when(mine)
        def _():
            def group(i, _):
                for k in range(8):
                    j = i * 8 + k
                    row = state_ref[pl.ds(cells_ref[b, band * quarter + j], 1), :]
                    rows_ref[pl.ds(t * quarter + j, 1), :] = jnp.where(lane == members + 3, value_ref[b, j], row)
                return 0

            lax.fori_loop(0, quarter // 8, group, 0)

        @pl.when(jnp.logical_not(mine))
        def _():
            rows_ref[pl.ds(pl.multiple_of(t * quarter, quarter), quarter), :] = jnp.zeros((quarter, LANES), F32)

        return 0

    lax.fori_loop(0, batches, batch, 0)
    slabs, height, chunk = packed_ref.shape
    for q in range(slabs):
        packed_ref[q] = rows_ref[pl.ds(q * chunk, chunk), :].T[:height]


def spread_kernel(bands, slabs, rows_ref, out_ref, land, send1, recv1, send2, recv2, send3, recv3, send4, recv4, send5, recv5):
    x, b = lax.axis_index("gx"), lax.axis_index("gy")
    partner = b + 1 - 2 * lax.rem(b, 2)
    across = lax.rem(b + 2, bands)

    def slab(k):
        return lax.rem(x + k, slabs)

    def source(k):
        return lax.rem(x + slabs - k, slabs)

    def first(k):
        return pltpu.make_async_remote_copy(
            src_ref=rows_ref.at[slab(k)], dst_ref=land.at[k], send_sem=send1.at[k], recv_sem=recv1.at[k],
            device_id={"gx": slab(k)}, device_id_type=MESH,
        )

    def second(k):
        return pltpu.make_async_remote_copy(
            src_ref=out_ref.at[b, x], dst_ref=out_ref.at[b, x], send_sem=send2.at[k],
            recv_sem=recv2.at[k], device_id={"gx": slab(k)}, device_id_type=MESH,
        )

    def hand(k, of_band, send_sem, recv_sem, target):
        place = out_ref.at[of_band, source(k)]
        return pltpu.make_async_remote_copy(
            src_ref=place, dst_ref=place, send_sem=send_sem.at[k], recv_sem=recv_sem.at[k],
            device_id={"gy": target}, device_id_type=MESH,
        )

    def third(k):
        return hand(k, b, send3, recv3, partner)

    def fourth(k):
        return hand(k, b, send4, recv4, across)

    def fifth(k):
        return hand(k, across, send5, recv5, partner)

    def each(low, high, body):
        def step(k, _):
            body(k)
            return 0

        lax.fori_loop(low, high, step, 0)

    barrier = pltpu.get_barrier_semaphore()
    each(1, slabs, lambda k: pl.semaphore_signal(barrier, inc=1, device_id={"gx": slab(k)}, device_id_type=MESH))
    for target in (partner, across):
        pl.semaphore_signal(barrier, inc=1, device_id={"gy": target}, device_id_type=MESH)
    pl.semaphore_wait(barrier, slabs + 1)

    each(1, slabs, lambda k: first(k).start())
    out_ref[b, x] = rows_ref[x]

    def add(k):
        first(k).wait_recv()
        out_ref[b, x] += land[k]

    each(1, slabs, add)
    fourth(0).start()
    each(1, slabs, lambda k: second(k).start())
    third(0).start()

    def relay(k):
        second(k).wait_recv()
        fourth(k).start()
        third(k).start()
        fourth(k - 1).wait_recv()
        fifth(k - 1).start()

    each(1, slabs, relay)
    fourth(slabs - 1).wait_recv()
    fifth(slabs - 1).start()

    def finish(k):
        third(k).wait()
        fifth(k).wait()
        fourth(k).wait_send()

    each(0, slabs, finish)

    def sent(k):
        first(k).wait_send()
        second(k).wait_send()

    each(1, slabs, sent)


def main_kernel(
    sizes, order_ref, owner_ref, state_ref, obs_ref, cell_ref, root_ref, gain_ref,
    anom_out, mean_out,
    lat_ref, lon_ref, cells_s, obs_s, v_s, vw_s, z3_s, gh_s, gl_s, send_sem, recv_sem,
):
    members, lon_dev, lat_dev, levels, lon_total, lat_total, span, bands = sizes
    batches, obs = cell_ref.shape
    quarter = obs // bands
    column, band = lax.axis_index("gx"), lax.axis_index("gy")
    classes = lon_dev * lat_dev
    chunk = 4

    barrier = pltpu.get_barrier_semaphore()
    for k in range(1, bands):
        pl.semaphore_signal(barrier, inc=1, device_id={"gy": lax.rem(band + k, bands)}, device_id_type=MESH)
    pl.semaphore_wait(barrier, bands - 1)

    def widen(value, with_low_in_middle):
        high, low = split(value)
        high, low = high.astype(F32), low.astype(F32)
        second, third = (low, high) if with_low_in_middle else (high, low)
        lane = lane_ids(value.shape)
        room = LANES - members
        moved = pltpu.roll(second, members, 1)
        first = jnp.where(lane < members, high, moved)
        last = jnp.where(lane < members - room, moved, pltpu.roll(third, members - room, 1))
        return jnp.concatenate([first, last], axis=1), lane, room

    def state_wide(value):
        return widen(value, True)[0].astype(BF16)

    def prior_wide(value):
        wide, lane, room = widen(jnp.where(lane_ids(value.shape) < members, value, 0.0), False)
        wide_lane = lane_ids(wide.shape)
        return jnp.where(wide_lane < 3 * members, wide, 0.0).astype(BF16)

    def lon_weight(gap):
        gap = jnp.abs(gap)
        gap = jnp.minimum(gap, lon_total - gap)
        return jnp.maximum(0.0, 1.0 - gap * (1.0 / span))

    def lat_weight(gap):
        return 1.0 - jnp.abs(gap) * (1.0 / lat_total)

    def obs_taper(rows, s):
        lat, lon = rows[:, members + 1:members + 2], rows[:, members + 2:members + 3]
        return lat_weight(lat - lat_ref[s]) * lon_weight(lon - lon_ref[s])

    def apply(rows, high, low):
        both = nn(high, vw_s[...])
        return rows - (both[:, :LANES] + both[:, LANES:] + nn(low, vw_s[:, :LANES]))

    def update(rows, taper, s, slot):
        gained = nt(state_wide(rows), z3_s[slot]) * taper
        return apply(rows, *split(gained))

    def update_cells(s, slot):
        for i in range(classes // chunk):
            tapers = []
            for k in range(chunk):
                c = i * chunk + k
                lat = (band * lat_dev + c % lat_dev).astype(F32)
                lon = (column * lon_dev + c // lat_dev).astype(F32)
                weight = lat_weight(lat - lat_ref[s]) * lon_weight(lon - lon_ref[s])
                tapers.append(jnp.broadcast_to(weight, (levels, obs)))
            here = pl.ds(i * chunk * levels, chunk * levels)
            cells_s[here, :] = update(cells_s[here, :], jnp.concatenate(tapers, axis=0), s, slot)

    def at(t):
        return pl.ds(pl.multiple_of(t * obs, obs), obs)

    cells_s[...] = state_ref[...]
    _, slabs, height, width = obs_ref.shape
    part = min(width, quarter)
    for q in range(bands):
        for p in range(slabs):
            rest = jnp.zeros((LANES - height, width), F32)
            block = jnp.concatenate([obs_ref[q, p], rest], axis=0).T
            for i in range(0, width, part):
                t, j = divmod(p * width + i, quarter)
                obs_s[pl.ds(t * obs + q * quarter + j, part), :] = block[i:i + part]
    obs_s[pl.ds(batches * obs, 2 * obs), :] = jnp.zeros((2 * obs, LANES), F32)
    vw_s[...] = jnp.zeros_like(vw_s)
    z3_s[...] = jnp.zeros_like(z3_s)
    first_lat = lax.broadcasted_iota(jnp.int32, (1, obs), 1).astype(F32)
    first_lat = jnp.floor((first_lat + 0.5) * (1.0 / quarter)) * lat_dev
    for t in range(batches):
        batch_id = order_ref[t]
        level_row = jnp.floor((cell_ref[pl.ds(batch_id, 1), :].astype(F32) + 0.5) * (1.0 / levels))
        lon_row = jnp.floor((level_row + 0.5) * (1.0 / lat_dev))
        lat_ref[t] = level_row - lon_row * lat_dev + first_lat
        lon_ref[t] = lon_row + (owner_ref[batch_id] * lon_dev).astype(F32)

    def turn(t, _):
        prior = obs_s[at(t), :]
        lane = lane_ids(prior.shape)
        innovation = pltpu.roll(prior, LANES - 3, 1) - prior
        joined = jnp.where(lane < members, prior, jnp.where(lane == members, innovation, 0.0))
        high, low = split(joined)
        batch_id = order_ref[t]
        table_high, table_low = split(jnp.concatenate([root_ref[batch_id], gain_ref[batch_id]], axis=0))
        both = nn(table_high, jnp.concatenate([high, low], axis=1))
        part = both[:, :LANES] + both[:, LANES:] + nn(table_low, high)
        lane = lane_ids((quarter, LANES))
        weighted = jnp.where(lane < members, part[:quarter], jnp.where(lane == members, -part[quarter:], 0.0))
        mine = pl.ds(pl.multiple_of(band * quarter, quarter), quarter)
        v_s[t, mine, :] = weighted * (1.0 / (members - 1.0))

        def copy(k):
            return pltpu.make_async_remote_copy(
                src_ref=v_s.at[t, mine, :],
                dst_ref=v_s.at[t, mine, :],
                send_sem=send_sem.at[t, k - 1],
                recv_sem=recv_sem.at[t, k - 1],
                device_id={"gy": lax.rem(band + k, bands)},
                device_id_type=MESH,
            )

        for k in range(1, bands):
            copy(k).start()

        z3_s[lax.rem(t, 2)] = prior_wide(prior)

        before = jnp.maximum(t - 1, 0)
        past = lax.rem(t + 1, 2)
        rows = obs_s[at(t + 1), :]
        rows = update(rows, obs_taper(rows, before), before, past)
        obs_s[at(t + 1), :] = rows
        gained = nt(state_wide(rows), z3_s[lax.rem(t, 2)]) * obs_taper(rows, t)
        gh_s[...], gl_s[...] = split(gained)
        update_cells(before, past)

        def later(i, _):
            here = pl.ds(pl.multiple_of((t + 2 + 2 * i) * obs, obs), 2 * obs)
            rows = obs_s[here, :]
            obs_s[here, :] = update(rows, obs_taper(rows, before), before, past)
            return 0

        lax.fori_loop(0, (batches - 1 - t) // 2 * jnp.minimum(t, 1), later, 0)

        for k in range(1, bands):
            copy(k).wait()

        vw_s[...] = jnp.concatenate(split(v_s[t]), axis=1)

        obs_s[at(t + 1), :] = apply(obs_s[at(t + 1), :], gh_s[...], gl_s[...])
        return 0

    lax.fori_loop(0, batches, turn, 0)
    update_cells(batches - 1, (batches - 1) % 2)
    for c in range(classes):
        tall = cells_s[pl.ds(c * levels, levels), :].T
        anom_out[:, c, :] = tall[:members]
        mean_out[pl.ds(c, 1), :] = tall[members:members + 1]


def local(anomalies, state_mean, obs_value, obs_cell, owner, order, root_inv, gain_inv):
    members, lon_dev, lat_dev, levels = anomalies.shape
    classes = lon_dev * lat_dev
    cells = classes * levels
    batches, quarter = obs_value.shape
    obs = obs_cell.shape[1]
    slabs, bands = lax.axis_size("gx"), lax.axis_size("gy")
    chunk = batches * quarter // slabs
    height = (members + 4 + 7) // 8 * 8
    state, rows = pl.pallas_call(
        functools.partial(pick_kernel, lon_dev, lat_dev),
        out_shape=(
            jax.ShapeDtypeStruct((cells, LANES), F32),
            jax.ShapeDtypeStruct((slabs, height, chunk), F32),
        ),
        in_specs=[SMEM] * 4 + [VMEM] * 2,
        out_specs=(VMEM, VMEM),
        scratch_shapes=[pltpu.VMEM((batches * quarter, LANES), F32)],
        name="pick",
    )(
        obs_cell, obs_value, owner, order,
        anomalies.reshape(members, classes, levels), state_mean.reshape(classes, levels),
    )

    rows = pl.pallas_call(
        functools.partial(spread_kernel, bands, slabs),
        out_shape=jax.ShapeDtypeStruct((bands, slabs, height, chunk), F32),
        in_specs=[VMEM],
        out_specs=VMEM,
        scratch_shapes=[pltpu.VMEM((slabs, height, chunk), F32)] + [pltpu.SemaphoreType.DMA((slabs,))] * 10,
        compiler_params=pltpu.CompilerParams(collective_id=1, has_side_effects=True),
        name="spread",
    )(rows)

    sizes = (
        members, lon_dev, lat_dev, levels, float(slabs * lon_dev), float(bands * lat_dev), REACH * lon_dev + 1.0, bands
    )
    post, mean = pl.pallas_call(
        functools.partial(main_kernel, sizes),
        out_shape=(
            jax.ShapeDtypeStruct((members, classes, levels), F32),
            jax.ShapeDtypeStruct((classes, levels), F32),
        ),
        in_specs=[SMEM] * 2 + [VMEM] * 5,
        out_specs=(VMEM, VMEM),
        scratch_shapes=[
            pltpu.VMEM((batches, 1, obs), F32),
            pltpu.VMEM((batches, 1, obs), F32),
            pltpu.VMEM((cells, LANES), F32),
            pltpu.VMEM(((batches + 2) * obs, LANES), F32),
            pltpu.VMEM((batches, obs, LANES), F32),
            pltpu.VMEM((obs, 2 * LANES), BF16),
            pltpu.VMEM((2, obs, 2 * LANES), BF16),
            pltpu.VMEM((obs, obs), BF16),
            pltpu.VMEM((obs, obs), BF16),
            pltpu.SemaphoreType.DMA((batches, bands - 1)),
            pltpu.SemaphoreType.DMA((batches, bands - 1)),
        ],
        compiler_params=pltpu.CompilerParams(collective_id=0, has_side_effects=True),
        name="analysis",
    )(
        order, owner, state, rows, obs_cell, root_inv, gain_inv,
    )
    return post.reshape(members, lon_dev, lat_dev, levels), mean.reshape(lon_dev, lat_dev, levels)


def solution(mesh):
    return jax.shard_map(
        local,
        mesh=mesh,
        in_specs=(
            P(None, "gx", "gy", None),
            P("gx", "gy", None),
            P(None, "gy"),
            P(),
            P(),
            P(),
            P(None, "gy", None),
            P(None, "gy", None),
        ),
        out_specs=(P(None, "gx", "gy", None), P("gx", "gy", None)),
        check_vma=False,
    )
```

profile of v0, /device:TPU:0, one launch (start us, length us, event | category | flops | bytes accessed | tf_op | source)
XLA Modules:
  0.0 125.0 jit_solution(13671221802035948060)
XLA Ops:
  0.6 4.3 %pick.1 = (f32[2048,128]{1,0:T(8,128)}, f32[8,88,128]{2,1,0:T(8,128)}) custom-call(s32[16,256]{1,0:T(8,128)} %cell_ref.1, f32[16,64]{1,0:T(8,128)} %value_ref.1, s32[16]{0:T(128)} %owner_ref.3, s32[16]{0:T(128)} %order_ref.3, f32[80,16,128]{2,1,0:T(8,128)} %bitcast.4, f32[16,128]{1,0:T(8,128)} %bitcast.6), custom_call_target="tpu_custom_call" | custom-call | tf_op jit(solution)/shard_map/pick/pallas_call | solution.py:339
  4.9 35.1 %spread.1.obs_ref = f32[4,8,88,128]{3,2,1,0:T(8,128)} custom-call(f32[8,88,128]{2,1,0:T(8,128)} %get-tuple-element.7.rows_ref), custom_call_target="tpu_custom_call" | custom-call | tf_op jit(solution)/shard_map/spread/pallas_call | solution.py:354
  40.0 81.7 %analysis.1 = (f32[80,16,128]{2,1,0:T(8,128)}, f32[16,128]{1,0:T(8,128)}) custom-call(s32[16]{0:T(128)} %order_ref.3, s32[16]{0:T(128)} %owner_ref.3, f32[2048,128]{1,0:T(8,128)} %get-tuple-element.6.state_ref, f32[4,8,88,128]{3,2,1,0:T(8,128)} %spread.1.obs_ref, s32[16,256]{1,0:T(8,128)} %cell_ref.1, f32[16,64,256]{2,1,0:T(8,128)} %root_ref.1, ...), custom_call_target="tpu_custom_call" | custom-call | tf_op jit(solution)/shard_map/analysis/pallas_call | solution.py:367
  121.7 2.0 %copy.12 = f32[80,2,8,128]{3,2,1,0:T(8,128)} copy(f32[80,2,8,128]{3,2,1,0:T(8,128)} %bitcast.5) | data formatting | bytes 1310720
  123.7 1.3 %copy.13 = f32[2,8,128]{2,1,0:T(8,128)} copy(f32[2,8,128]{2,1,0:T(8,128)} %bitcast.7) | data formatting | bytes 16384
where the time goes:
time: 127 us; the launch traced here: 125 us
  Pallas kernels  121 us (95%)
  local copies, waits for them, and re-layouts  3.26 us (3%)
    pallas_call x1, Pallas kernels, local(): pl.pallas_call(functools.partial(main_kernel, sizes), out_shape=(jax.Shap...  81.7 us
    pallas_call x1, Pallas kernels, local(): pl.pallas_call(functools.partial(spread_kernel, bands, slabs), out_shape=...  35.1 us
    pallas_call x1, Pallas kernels, local(): pl.pallas_call(functools.partial(pick_kernel, lon_dev, lat_dev), out_shap...  4.26 us
    unnamed x2, local copies, waits for them, and re-layouts  3.26 us

commit v1 on v0

--- a/solution.py
+++ b/solution.py
@@ -8,6 +8,7 @@
 from jax.sharding import PartitionSpec as P
 
 REACH = 3
+EARLY = 5
 LANES = 128
 MESH = pl.DeviceIdType.MESH
 VMEM = pl.BlockSpec(memory_space=pltpu.VMEM)
@@ -327,7 +328,7 @@
         mean_out[pl.ds(c, 1), :] = tall[members:members + 1]
 
 
-def local(anomalies, state_mean, obs_value, obs_cell, owner, order, root_inv, gain_inv):
+def wide_local(anomalies, state_mean, obs_value, obs_cell, owner, order, root_inv, gain_inv):
     members, lon_dev, lat_dev, levels = anomalies.shape
     classes = lon_dev * lat_dev
     cells = classes * levels
@@ -393,6 +394,467 @@
     return post.reshape(members, lon_dev, lat_dev, levels), mean.reshape(lon_dev, lat_dev, levels)
 
 
+def arrange_kernel(
+    lon_dev, lat_dev, lat_total, cells_ref, value_ref, owner_ref, order_ref, anom_ref, mean_ref, root_ref, gain_ref,
+    state_ref, packed_ref, table_ref,
+):
+    column, band = lax.axis_index("gx"), lax.axis_index("gy")
+    members, classes, levels = anom_ref.shape
+    batches, quarter = value_ref.shape
+    slabs, height, _ = packed_ref.shape
+    piece = height // batches
+    half = table_ref.shape[-1]
+
+    for c in range(classes):
+        lat = (band * lat_dev + c % lat_dev).astype(F32) * (1.0 / lat_total)
+        lon = (column * lon_dev + c // lat_dev).astype(F32)
+        tall = jnp.concatenate(
+            [
+                anom_ref[:, c, :],
+                mean_ref[pl.ds(c, 1), :],
+                jnp.full((1, levels), lat, F32),
+                jnp.full((1, levels), lon, F32),
+                jnp.zeros((1, levels), F32),
+                jnp.full((1, levels), float(c // lat_dev), F32),
+                jnp.zeros((LANES - members - 5, levels), F32),
+            ],
+            axis=0,
+        )
+        state_ref[pl.ds(c * levels, levels), :] = tall.T
+
+    lane = lane_ids((1, LANES))
+
+    def batch(t, _):
+        b = order_ref[t]
+        mine = owner_ref[b] == column
+        for h in range(2):
+            table_ref[t, 0, h] = root_ref[b, :, h * half:(h + 1) * half]
+            table_ref[t, 1, h] = gain_ref[b, :, h * half:(h + 1) * half]
+
+        @pl.when(mine)
+        def _():
+            def group(p, _):
+                for k in range(piece):
+                    j = p * piece + k
+                    row = state_ref[pl.ds(cells_ref[b, band * quarter + j], 1), :]
+                    packed_ref[p, pl.ds(t * piece + k, 1), :] = jnp.where(lane == members + 3, value_ref[b, j], row)
+                return 0
+
+            lax.fori_loop(0, slabs, group, 0)
+
+        @pl.when(jnp.logical_not(mine))
+        def _():
+            here = pl.ds(pl.multiple_of(t * piece, piece), piece)
+            packed_ref[:, here, :] = jnp.zeros((slabs, piece, LANES), F32)
+
+        return 0
+
+    lax.fori_loop(0, batches, batch, 0)
+
+
+def analysis_kernel(
+    sizes, order_ref, owner_ref, state_ref, packed_ref, table_ref, cell_ref,
+    cells_s,
+    lat_ref, lon_ref, land, mine_s, share_s, obs_s, full_s, th_s, tl_s, z3_s, vw_s,
+    rs_send, rs_recv, send1, recv1, send2, recv2, near_send, near_recv, far_send, far_recv, hand_send, hand_recv, own_sem,
+):
+    members, lon_dev, lat_dev, levels, lon_total, lat_total, span, bands, slabs, early = sizes
+    batches, obs = cell_ref.shape
+    quarter, half = obs // bands, obs // 2
+    piece = quarter // slabs
+    ahead, first_tables = min(5, batches), min(3, batches)
+    column, band = lax.axis_index("gx"), lax.axis_index("gy")
+    partner = band + 1 - 2 * lax.rem(band, 2)
+    across = lax.rem(band + bands // 2, bands)
+    near = lax.div(band, bands // 2)
+    far = 1 - near
+    classes = lon_dev * lat_dev
+    chunk = 4
+
+    def slab(k):
+        return lax.rem(column + k, slabs)
+
+    def band_rows(b):
+        return pl.ds(pl.multiple_of(b * quarter, quarter), quarter)
+
+    def half_rows(h):
+        return pl.ds(pl.multiple_of(h * half, half), half)
+
+    def remote(src, dst, send, recv, device):
+        return pltpu.make_async_remote_copy(
+            src_ref=src, dst_ref=dst, send_sem=send, recv_sem=recv, device_id=device, device_id_type=MESH
+        )
+
+    parts = ((0, early * piece), (early * piece, (batches - early) * piece))
+
+    def reduce_copy(k, p):
+        here = pl.ds(*parts[p])
+        return remote(
+            packed_ref.at[slab(k), here], land.at[k, here], rs_send.at[p, k], rs_recv.at[p, k], {"gx": slab(k)}
+        )
+
+    def my_piece(s):
+        return pl.ds(pl.multiple_of(s * piece, piece), piece)
+
+    def my_place():
+        return pl.ds(pl.multiple_of(band * quarter + column * piece, piece), piece)
+
+    def share(s):
+        rows = mine_s[my_piece(s), :]
+        share_s[s] = rows
+        obs_s[s, my_place(), :] = rows
+
+        def start(device):
+            remote(share_s.at[s], obs_s.at[s, my_place()], send1.at[s], recv1.at[s], device).start()
+
+        for k in range(1, slabs):
+            start({"gx": slab(k)})
+        for k in range(slabs):
+            start({"gx": slab(k), "gy": across})
+
+    def shared(s, sem):
+        window = obs_s.at[s, pl.ds(0, (2 * slabs - 1) * piece)]
+        pltpu.make_async_copy(window, window, sem.at[s]).wait()
+
+    def pass_on(s, i):
+        place = obs_s.at[s, band_rows((band, across)[i])]
+        return remote(place, place, send2.at[s, i], recv2.at[s, i], {"gy": partner})
+
+    def near_copy(t):
+        return remote(
+            table_ref.at[t], full_s.at[t, :, :, band_rows(band)], near_send.at[t], near_recv.at[t], {"gy": partner}
+        )
+
+    def far_copy(t):
+        return remote(
+            table_ref.at[t, :, near], full_s.at[t, :, near, band_rows(band)], far_send.at[t], far_recv.at[t],
+            {"gy": across},
+        )
+
+    def hand_copy(t):
+        place = full_s.at[t, :, far, band_rows(across)]
+        return remote(place, place, hand_send.at[t], hand_recv.at[t], {"gy": partner})
+
+    def send_table(t):
+        far_copy(t).start()
+        near_copy(t).start()
+
+    def hand_table(t):
+        far_copy(t).wait_recv()
+        hand_copy(t).start()
+
+    def own_tables():
+        return pltpu.make_async_copy(table_ref, full_s.at[:, :, :, band_rows(band)], own_sem)
+
+    def prepare(t, slot):
+        for k in range(2):
+            aside = full_s[t, k, far, half_rows(near), :]
+            blocks = (
+                (near, near, full_s[t, k, near, half_rows(near), :]),
+                (far, near, aside),
+                (near, far, aside.T),
+                (far, far, full_s[t, k, far, half_rows(far), :]),
+            )
+            for columns, rows, block in blocks:
+                here = pl.ds(pl.multiple_of(k * obs + rows * half, half), half)
+                high, low = split(block)
+                th_s[slot, columns, here, :] = high
+                tl_s[slot, columns, here, :] = low
+
+    barrier = pltpu.get_barrier_semaphore()
+    for k in range(1, slabs):
+        pl.semaphore_signal(barrier, inc=1, device_id={"gx": slab(k)}, device_id_type=MESH)
+    for k in range(slabs):
+        pl.semaphore_signal(barrier, inc=1, device_id={"gx": slab(k), "gy": across}, device_id_type=MESH)
+    pl.semaphore_signal(barrier, inc=1, device_id={"gy": partner}, device_id_type=MESH)
+    pl.semaphore_wait(barrier, 2 * slabs)
+
+    for p in range(2):
+        for k in range(1, slabs):
+            reduce_copy(k, p).start()
+        if p == 0:
+            own_tables().start()
+            for t in range(first_tables):
+                send_table(t)
+
+    first_lat = lax.broadcasted_iota(jnp.int32, (1, obs), 1).astype(F32)
+    first_lat = jnp.floor((first_lat + 0.5) * (1.0 / quarter)) * lat_dev
+    for t in range(batches):
+        batch_id = order_ref[t]
+        level_row = jnp.floor((cell_ref[pl.ds(batch_id, 1), :].astype(F32) + 0.5) * (1.0 / levels))
+        lon_row = jnp.floor((level_row + 0.5) * (1.0 / lat_dev))
+        lat_ref[t + early] = (level_row - lon_row * lat_dev + first_lat) * (1.0 / lat_total)
+        lon_ref[t + early] = lon_row + (owner_ref[batch_id] * lon_dev).astype(F32)
+    for t in range(early):
+        lat_ref[t] = jnp.zeros((1, obs), F32)
+        lon_ref[t] = jnp.zeros((1, obs), F32)
+        vw_s[t] = jnp.zeros(vw_s.shape[1:], BF16)
+        z3_s[t] = jnp.zeros(z3_s.shape[1:], BF16)
+    for s in range(batches, obs_s.shape[0]):
+        obs_s[s] = jnp.zeros(obs_s.shape[1:], F32)
+    cells_s[...] = state_ref[...]
+
+    def collect(p):
+        here = pl.ds(*parts[p])
+        total = packed_ref[column, here, :]
+        for k in range(1, slabs):
+            reduce_copy(k, p).wait_recv()
+            total = total + land[k, here, :]
+        mine_s[here, :] = total
+
+    collect(0)
+    for s in range(early):
+        share(s)
+    for t in range(first_tables, ahead):
+        send_table(t)
+    for t in range(min(3, batches)):
+        hand_table(t)
+    collect(1)
+    for s in range(early):
+        shared(s, recv1)
+        for i in range(2):
+            pass_on(s, i).start()
+    own_tables().wait()
+    near_copy(0).wait_recv()
+    hand_copy(0).wait_recv()
+    prepare(0, 0)
+    for s in range(early):
+        for i in range(2):
+            pass_on(s, i).wait()
+
+    def state_wide(value):
+        high, low = split(value)
+        high, low = high.astype(F32), low.astype(F32)
+        lane = lane_ids(value.shape)
+        room = LANES - members
+        moved = pltpu.roll(low, members, 1)
+        first = jnp.where(lane < members, high, moved)
+        last = jnp.where(lane < members - room, moved, pltpu.roll(high, members - room, 1))
+        return jnp.concatenate([first, last], axis=1).astype(BF16)
+
+    def prior_tall(prior):
+        high, low = split(prior.T[:members])
+        return jnp.concatenate([high, high, low, jnp.zeros((2 * LANES - 3 * members, obs), BF16)], axis=0)
+
+    def lon_weight(gap):
+        gap = jnp.abs(gap)
+        gap = jnp.minimum(gap, lon_total - gap)
+        return jnp.maximum(0.0, 1.0 - gap * (1.0 / span))
+
+    def lat_weight(gap):
+        return 1.0 - jnp.abs(gap)
+
+    def apply(rows, high, low, e):
+        both = nn(high, vw_s[e])
+        return rows - (both[:, :LANES] + both[:, LANES:] + nn(low, vw_s[e, :, :LANES]))
+
+    def gain_of(rows, taper, e):
+        return split(nn(state_wide(rows), z3_s[e]) * taper)
+
+    def update(rows, taper, e):
+        high, low = gain_of(rows, taper, e)
+        return apply(rows, high, low, e)
+
+    def obs_taper(lat, bit, s, e):
+        lon = (owner_ref[order_ref[jnp.minimum(s, batches - 1)]] * lon_dev).astype(F32)
+        west = lon_weight(lon - lon_ref[e])
+        east = lon_weight(lon + 1.0 - lon_ref[e])
+        return lat_weight(lat - lat_ref[e]) * (west + bit * (east - west))
+
+    def update_mine(e):
+        rows = mine_s[...]
+        lat, lon = rows[:, members + 1:members + 2], rows[:, members + 2:members + 3]
+        taper = lat_weight(lat - lat_ref[e]) * lon_weight(lon - lon_ref[e])
+        mine_s[...] = update(rows, taper, e)
+
+    def update_cells(e):
+        for i in range(classes // chunk):
+            tapers = []
+            for k in range(chunk):
+                c = i * chunk + k
+                lat = (band * lat_dev + c % lat_dev).astype(F32) * (1.0 / lat_total)
+                lon = (column * lon_dev + c // lat_dev).astype(F32)
+                weight = lat_weight(lat - lat_ref[e]) * lon_weight(lon - lon_ref[e])
+                tapers.append(jnp.broadcast_to(weight, (levels, obs)))
+            here = pl.ds(i * chunk * levels, chunk * levels)
+            cells_s[here, :] = update(cells_s[here, :], jnp.concatenate(tapers, axis=0), e)
+
+    def columns_of(rows):
+        return rows[:, members + 1:members + 2], rows[:, members + 4:members + 5]
+
+    def turn(t, _):
+        slot = lax.rem(t, 2)
+        e = t + early
+
+        @pl.when(e < batches)
+        def _():
+            share(e)
+
+        passing = e - 2
+
+        @pl.when(jnp.logical_and(passing >= early, passing < batches))
+        def _():
+            shared(passing, recv1)
+            for i in range(2):
+                pass_on(passing, i).start()
+
+        @pl.when(t + ahead < batches)
+        def _():
+            send_table(t + ahead)
+
+        @pl.when(t + 3 < batches)
+        def _():
+            hand_table(t + 3)
+
+        @pl.when(t + 1 < batches)
+        def _():
+            near_copy(t + 1).wait_recv()
+            hand_copy(t + 1).wait_recv()
+
+        coming = t + 2
+
+        @pl.when(jnp.logical_and(coming >= early, coming < batches))
+        def _():
+            for i in range(2):
+                pass_on(coming, i).wait()
+
+        prior = obs_s[t]
+        z3_s[e] = prior_tall(prior)
+        lane = lane_ids(prior.shape)
+        innovation = pltpu.roll(prior, LANES - 3, 1) - prior
+        joined = jnp.where(lane < members, prior, jnp.where(lane == members, innovation, 0.0))
+        high, low = split(joined)
+        table_high = jnp.concatenate([th_s[slot, 0], th_s[slot, 1]], axis=1)
+        table_low = jnp.concatenate([tl_s[slot, 0], tl_s[slot, 1]], axis=1)
+        both = nn(table_high, jnp.concatenate([high, low], axis=1))
+        part = both[:, :LANES] + both[:, LANES:] + nn(table_low, high)
+        lane = lane_ids((obs, LANES))
+        weighted = jnp.where(lane < members, part[:obs], jnp.where(lane == members, -part[obs:], 0.0))
+        vw_s[e] = jnp.concatenate(split(weighted * (1.0 / (members - 1.0))), axis=1)
+
+        rows = obs_s[t + 1]
+        lat, bit = columns_of(rows)
+        gained = gain_of(rows, obs_taper(lat, bit, t + 1, e), e)
+
+        update_cells(e - 1)
+
+        obs_s[t + 1] = apply(rows, *gained, e)
+        update_mine(e)
+
+        rows = obs_s[t + 2]
+        lat, bit = columns_of(rows)
+        for k in range(early - 2, -1, -1):
+            rows = update(rows, obs_taper(lat, bit, t + 2, e - k), e - k)
+        obs_s[t + 2] = rows
+
+        prepare(jnp.minimum(t + 1, batches - 1), 1 - slot)
+        return 0
+
+    lax.fori_loop(0, batches, turn, 0)
+    update_cells(batches - 1 + early)
+
+    for p in range(2):
+        for k in range(1, slabs):
+            reduce_copy(k, p).wait_send()
+
+    def sent(t, _):
+        shared(t, send1)
+        near_copy(t).wait_send()
+        far_copy(t).wait_send()
+        hand_copy(t).wait_send()
+        return 0
+
+    lax.fori_loop(0, batches, sent, 0)
+
+
+def finish_kernel(cells_ref, anom_out, mean_out):
+    members, classes, levels = anom_out.shape
+    for c in range(classes):
+        tall = cells_ref[pl.ds(c * levels, levels), :].T
+        anom_out[:, c, :] = tall[:members]
+        mean_out[pl.ds(c, 1), :] = tall[members:members + 1]
+
+
+def near_local(anomalies, state_mean, obs_value, obs_cell, owner, order, root_inv, gain_inv):
+    members, lon_dev, lat_dev, levels = anomalies.shape
+    classes = lon_dev * lat_dev
+    cells = classes * levels
+    batches, quarter = obs_value.shape
+    obs = obs_cell.shape[1]
+    half = obs // 2
+    slabs, bands = lax.axis_size("gx"), lax.axis_size("gy")
+    piece = quarter // slabs
+    early = min(EARLY, batches)
+    lat_total = float(bands * lat_dev)
+    state, packed, table = pl.pallas_call(
+        functools.partial(arrange_kernel, lon_dev, lat_dev, lat_total),
+        out_shape=(
+            jax.ShapeDtypeStruct((cells, LANES), F32),
+            jax.ShapeDtypeStruct((slabs, batches * piece, LANES), F32),
+            jax.ShapeDtypeStruct((batches, 2, 2, quarter, half), F32),
+        ),
+        in_specs=[SMEM] * 4 + [VMEM] * 4,
+        out_specs=(VMEM, VMEM, VMEM),
+        name="arrange",
+    )(
+        obs_cell, obs_value, owner, order,
+        anomalies.reshape(members, classes, levels), state_mean.reshape(classes, levels), root_inv, gain_inv,
+    )
+
+    sizes = (
+        members, lon_dev, lat_dev, levels, float(slabs * lon_dev), lat_total, REACH * lon_dev + 1.0, bands, slabs, early
+    )
+    dma = pltpu.SemaphoreType.DMA
+    cells_out = pl.pallas_call(
+        functools.partial(analysis_kernel, sizes),
+        out_shape=jax.ShapeDtypeStruct((cells, LANES), F32),
+        in_specs=[SMEM] * 2 + [VMEM] * 4,
+        out_specs=VMEM,
+        scratch_shapes=[
+            pltpu.VMEM((batches + early, 1, obs), F32),
+            pltpu.VMEM((batches + early, 1, obs), F32),
+            pltpu.VMEM((slabs, batches * piece, LANES), F32),
+            pltpu.VMEM((batches * piece, LANES), F32),
+            pltpu.VMEM((batches, piece, LANES), F32),
+            pltpu.VMEM((batches + 2, obs, LANES), F32),
+            pltpu.VMEM((batches, 2, 2, obs, half), F32),
+            pltpu.VMEM((2, 2, 2 * obs, half), BF16),
+            pltpu.VMEM((2, 2, 2 * obs, half), BF16),
+            pltpu.VMEM((batches + early, 2 * LANES, obs), BF16),
+            pltpu.VMEM((batches + early, obs, 2 * LANES), BF16),
+            dma((2, slabs)), dma((2, slabs)),
+            dma((batches,)), dma((batches,)),
+            dma((batches, 2)), dma((batches, 2)),
+            dma((batches,)), dma((batches,)),
+            dma((batches,)), dma((batches,)),
+            dma((batches,)), dma((batches,)),
+            dma,
+        ],
+        compiler_params=pltpu.CompilerParams(collective_id=0, has_side_effects=True),
+        name="analysis",
+    )(order, owner, state, packed, table, obs_cell)
+
+    post, mean = pl.pallas_call(
+        finish_kernel,
+        out_shape=(
+            jax.ShapeDtypeStruct((members, classes, levels), F32),
+            jax.ShapeDtypeStruct((classes, levels), F32),
+        ),
+        in_specs=[VMEM],
+        out_specs=(VMEM, VMEM),
+        name="finish",
+    )(cells_out)
+    return post.reshape(members, lon_dev, lat_dev, levels), mean.reshape(lon_dev, lat_dev, levels)
+
+
+def local(*arrays):
+    obs_value, obs_cell = arrays[2], arrays[3]
+    slabs, bands = lax.axis_size("gx"), lax.axis_size("gy")
+    piece = obs_value.shape[1] // slabs
+    fits = bands == 4 and piece % 8 == 0 and piece * slabs == obs_value.shape[1] and obs_cell.shape[1] == 2 * LANES
+    return (near_local if fits and arrays[0].shape[1] == 2 else wide_local)(*arrays)
+
+
 def solution(mesh):
     return jax.shard_map(
         local,

time: 127 us -> 92.7 us (0.73); the launches traced: 125 us -> 92.5 us
  Pallas kernels: 121 us -> 91.9 us
  local copies, waits for them, and re-layouts: 3.26 us -> 0 us
    pallas_call x3, Pallas kernels: 121 us -> 91.9 us  [the longest x1 83.9 us: near_local(): pl.pallas_call(functools.partial(analysis_kernel, sizes), out_shape=jax.S...]
    unnamed x2 -> x0, local copies, waits for them, and re-layouts: 3.26 us -> none
where the time goes in v1:
time: 92.7 us; the launch traced here: 92.5 us
  Pallas kernels  91.9 us (99%)
    pallas_call x1, Pallas kernels, near_local(): pl.pallas_call(functools.partial(analysis_kernel, sizes), out_shape=jax.S...  83.9 us
    pallas_call x1, Pallas kernels, near_local(): pl.pallas_call(functools.partial(arrange_kernel, lon_dev, lat_dev, lat_to...  5.44 us
    pallas_call x1, Pallas kernels, near_local(): pl.pallas_call(finish_kernel, out_shape=(jax.ShapeDtypeStruct((members, c...  2.51 us

profile of v1, /device:TPU:0, one launch (start us, length us, event | category | flops | bytes accessed | tf_op | source)
XLA Modules:
  0.0 92.5 jit_solution(246950480174373748)
XLA Ops:
  0.6 5.4 %arrange.1 = (f32[2048,128]{1,0:T(8,128)}, f32[8,128,128]{2,1,0:T(8,128)}, f32[16,2,2,64,128]{4,3,2,1,0:T(8,128)}) custom-call(s32[16,256]{1,0:T(8,128)} %cell_ref.1, f32[16,64]{1,0:T(8,128)} %value_ref.1, s32[16]{0:T(128)} %owner_ref.3, s32[16]{0:T(128)} %order_ref.3, f32[80,16,128]{2,1,0:T(8,128)} %bitcast.4, f32[16,128]{1,0:T(8,128)} %bitcast.5, ...), custom_call_target="tpu_custom_call" | custom-call | tf_op jit(solution)/shard_map/arrange/pallas_call | solution.py:789
  6.1 83.9 %analysis.1.cells_ref = f32[2048,128]{1,0:T(8,128)} custom-call(s32[16]{0:T(128)} %order_ref.3, s32[16]{0:T(128)} %owner_ref.3, f32[2048,128]{1,0:T(8,128)} %get-tuple-element.7.state_ref, f32[8,128,128]{2,1,0:T(8,128)} %get-tuple-element.8.packed_ref, f32[16,2,2,64,128]{4,3,2,1,0:T(8,128)} %get-tuple-element.9.table_ref, s32[16,256]{1,0:T(8,128)} %cell_ref.1), custom_call_target="tpu_custom_call" | custom-call | tf_op jit(solution)/shard_map/analysis/pallas_call | solution.py:808
  90.0 2.5 %finish.1 = (f32[80,16,128]{2,1,0:T(8,128)}, f32[16,128]{1,0:T(8,128)}) custom-call(f32[2048,128]{1,0:T(8,128)} %analysis.1.cells_ref), custom_call_target="tpu_custom_call" | custom-call | tf_op jit(solution)/shard_map/finish/pallas_call | solution.py:837

commit v2 on v1

--- a/solution.py
+++ b/solution.py
@@ -394,16 +394,140 @@
     return post.reshape(members, lon_dev, lat_dev, levels), mean.reshape(lon_dev, lat_dev, levels)
 
 
-def arrange_kernel(
-    lon_dev, lat_dev, lat_total, cells_ref, value_ref, owner_ref, order_ref, anom_ref, mean_ref, root_ref, gain_ref,
-    state_ref, packed_ref, table_ref,
+def analysis_kernel(
+    sizes, index_ref, order_ref, owner_ref, cell_ref, value_ref, anom_ref, mean_ref, root_ref, gain_ref,
+    cells_s,
+    lat_ref, lon_ref, pick_s, packed_s, land, mine_s, share_s, obs_s, full_s, th_s, tl_s, z3_s, vw_s,
+    rs_send, rs_recv, send1, recv1, send2, recv2, send3, recv3, near_send, near_recv, far_send, far_recv, hand_send, hand_recv,
 ):
+    members, lon_dev, lat_dev, levels, lon_total, lat_total, span, bands, slabs, early = sizes
+    batches, obs = cell_ref.shape
+    quarter, half = obs // bands, obs // 2
+    piece = quarter // slabs
+    ahead = min(5, batches)
     column, band = lax.axis_index("gx"), lax.axis_index("gy")
-    members, classes, levels = anom_ref.shape
-    batches, quarter = value_ref.shape
-    slabs, height, _ = packed_ref.shape
-    piece = height // batches
-    half = table_ref.shape[-1]
+    partner = band + 1 - 2 * lax.rem(band, 2)
+    across = lax.rem(band + bands // 2, bands)
+    near = lax.div(band, bands // 2)
+    far = 1 - near
+    classes = lon_dev * lat_dev
+    chunk = 4
+
+    def slab(k):
+        return lax.rem(column + k, slabs)
+
+    def band_rows(b):
+        return pl.ds(pl.multiple_of(b * quarter, quarter), quarter)
+
+    def half_rows(h):
+        return pl.ds(pl.multiple_of(h * half, half), half)
+
+    def remote(src, dst, send, recv, device):
+        return pltpu.make_async_remote_copy(
+            src_ref=src, dst_ref=dst, send_sem=send, recv_sem=recv, device_id=device, device_id_type=MESH
+        )
+
+    ends = (0, 3, early + 2, batches)
+
+    def part_rows(p):
+        return pl.ds(ends[p] * piece, (ends[p + 1] - ends[p]) * piece)
+
+    def reduce_copy(k, p):
+        here = part_rows(p)
+        return remote(
+            packed_s.at[slab(k), here], land.at[k, here], rs_send.at[p, k], rs_recv.at[p, k], {"gx": slab(k)}
+        )
+
+    def my_piece(s):
+        return pl.ds(pl.multiple_of(s * piece, piece), piece)
+
+    rank, side = lax.div(column, 2), lax.rem(column, 2)
+    ranks = slabs // 2
+
+    def keep(s):
+        rows = mine_s[my_piece(s), :]
+        share_s[s] = rows
+        obs_s[s, band, rank, side] = rows
+
+        def start(device):
+            remote(share_s.at[s], obs_s.at[s, band, rank, side], send1.at[s], recv1.at[s], device).start()
+
+        return start
+
+    def share_ranks(s):
+        start = keep(s)
+        for k in range(1, ranks):
+            start({"gx": 2 * lax.rem(rank + k, ranks) + side})
+
+    def share_sides(s):
+        pieces(s, ranks - 1, recv1)
+        place = obs_s.at[s, band, :, side]
+        for target in ({"gx": 2 * rank + 1 - side}, {"gy": across}, {"gx": 2 * rank + 1 - side, "gy": across}):
+            remote(place, place, send3.at[s], recv3.at[s], target).start()
+
+    def share(s):
+        start = keep(s)
+
+        for k in range(1, slabs):
+            start({"gx": slab(k)})
+        for k in range(slabs):
+            start({"gx": slab(k), "gy": across})
+
+    def pieces(s, count, sem):
+        window = mine_s.at[pl.ds(0, count * piece)]
+        pltpu.make_async_copy(window, window, sem.at[s]).wait()
+
+    def shared(s, sem):
+        pieces(s, 2 * slabs - 1, sem)
+
+    def pass_on(s, i):
+        place = obs_s.at[s, (band, across)[i]]
+        return remote(place, place, send2.at[s, i], recv2.at[s, i], {"gy": partner})
+
+    def near_copy(t):
+        return remote(
+            full_s.at[t, :, :, band_rows(band)], full_s.at[t, :, :, band_rows(band)], near_send.at[t], near_recv.at[t], {"gy": partner}
+        )
+
+    def far_copy(t):
+        return remote(
+            full_s.at[t, :, near, band_rows(band)], full_s.at[t, :, near, band_rows(band)], far_send.at[t],
+            far_recv.at[t], {"gy": across},
+        )
+
+    def hand_copy(t):
+        place = full_s.at[t, :, far, band_rows(across)]
+        return remote(place, place, hand_send.at[t], hand_recv.at[t], {"gy": partner})
+
+    def send_table(t):
+        far_copy(t).start()
+        near_copy(t).start()
+
+    def hand_table(t):
+        far_copy(t).wait_recv()
+        hand_copy(t).start()
+
+    def prepare(t, slot):
+        for k in range(2):
+            aside = full_s[t, k, far, half_rows(near), :]
+            blocks = (
+                (near, near, full_s[t, k, near, half_rows(near), :]),
+                (far, near, aside),
+                (near, far, aside.T),
+                (far, far, full_s[t, k, far, half_rows(far), :]),
+            )
+            for columns, rows, block in blocks:
+                here = pl.ds(pl.multiple_of(k * obs + rows * half, half), half)
+                high, low = split(block)
+                th_s[slot, columns, here, :] = high
+                tl_s[slot, columns, here, :] = low
+
+    barrier = pltpu.get_barrier_semaphore()
+    for k in range(1, slabs):
+        pl.semaphore_signal(barrier, inc=1, device_id={"gx": slab(k)}, device_id_type=MESH)
+    for k in range(slabs):
+        pl.semaphore_signal(barrier, inc=1, device_id={"gx": slab(k), "gy": across}, device_id_type=MESH)
+    pl.semaphore_signal(barrier, inc=1, device_id={"gy": partner}, device_id_type=MESH)
 
     for c in range(classes):
         lat = (band * lat_dev + c % lat_dev).astype(F32) * (1.0 / lat_total)
@@ -420,162 +544,39 @@
             ],
             axis=0,
         )
-        state_ref[pl.ds(c * levels, levels), :] = tall.T
-
-    lane = lane_ids((1, LANES))
-
-    def batch(t, _):
+        cells_s[pl.ds(c * levels, levels), :] = tall.T
+
+    def pick(t, _):
         b = order_ref[t]
-        mine = owner_ref[b] == column
-        for h in range(2):
-            table_ref[t, 0, h] = root_ref[b, :, h * half:(h + 1) * half]
-            table_ref[t, 1, h] = gain_ref[b, :, h * half:(h + 1) * half]
-
-        @pl.when(mine)
-        def _():
-            def group(p, _):
-                for k in range(piece):
-                    j = p * piece + k
-                    row = state_ref[pl.ds(cells_ref[b, band * quarter + j], 1), :]
-                    packed_ref[p, pl.ds(t * piece + k, 1), :] = jnp.where(lane == members + 3, value_ref[b, j], row)
-                return 0
-
-            lax.fori_loop(0, slabs, group, 0)
-
-        @pl.when(jnp.logical_not(mine))
-        def _():
-            here = pl.ds(pl.multiple_of(t * piece, piece), piece)
-            packed_ref[:, here, :] = jnp.zeros((slabs, piece, LANES), F32)
-
+        for j in range(quarter):
+            pick_s[pl.ds(j, 1), :] = cells_s[pl.ds(index_ref[b, band * quarter + j], 1), :]
+        block = pick_s[...]
+        values = jnp.broadcast_to(value_ref[pl.ds(b, 1), :], (LANES, quarter)).T
+        block = jnp.where(lane_ids(block.shape) == members + 3, values, block)
+        block = jnp.where(owner_ref[b] == column, block, 0.0)
+        packed_s[:, my_piece(t), :] = block.reshape(slabs, piece, LANES)
         return 0
 
-    lax.fori_loop(0, batches, batch, 0)
-
-
-def analysis_kernel(
-    sizes, order_ref, owner_ref, state_ref, packed_ref, table_ref, cell_ref,
-    cells_s,
-    lat_ref, lon_ref, land, mine_s, share_s, obs_s, full_s, th_s, tl_s, z3_s, vw_s,
-    rs_send, rs_recv, send1, recv1, send2, recv2, near_send, near_recv, far_send, far_recv, hand_send, hand_recv, own_sem,
-):
-    members, lon_dev, lat_dev, levels, lon_total, lat_total, span, bands, slabs, early = sizes
-    batches, obs = cell_ref.shape
-    quarter, half = obs // bands, obs // 2
-    piece = quarter // slabs
-    ahead, first_tables = min(5, batches), min(3, batches)
-    column, band = lax.axis_index("gx"), lax.axis_index("gy")
-    partner = band + 1 - 2 * lax.rem(band, 2)
-    across = lax.rem(band + bands // 2, bands)
-    near = lax.div(band, bands // 2)
-    far = 1 - near
-    classes = lon_dev * lat_dev
-    chunk = 4
-
-    def slab(k):
-        return lax.rem(column + k, slabs)
-
-    def band_rows(b):
-        return pl.ds(pl.multiple_of(b * quarter, quarter), quarter)
-
-    def half_rows(h):
-        return pl.ds(pl.multiple_of(h * half, half), half)
-
-    def remote(src, dst, send, recv, device):
-        return pltpu.make_async_remote_copy(
-            src_ref=src, dst_ref=dst, send_sem=send, recv_sem=recv, device_id=device, device_id_type=MESH
-        )
-
-    parts = ((0, early * piece), (early * piece, (batches - early) * piece))
-
-    def reduce_copy(k, p):
-        here = pl.ds(*parts[p])
-        return remote(
-            packed_ref.at[slab(k), here], land.at[k, here], rs_send.at[p, k], rs_recv.at[p, k], {"gx": slab(k)}
-        )
-
-    def my_piece(s):
-        return pl.ds(pl.multiple_of(s * piece, piece), piece)
-
-    def my_place():
-        return pl.ds(pl.multiple_of(band * quarter + column * piece, piece), piece)
-
-    def share(s):
-        rows = mine_s[my_piece(s), :]
-        share_s[s] = rows
-        obs_s[s, my_place(), :] = rows
-
-        def start(device):
-            remote(share_s.at[s], obs_s.at[s, my_place()], send1.at[s], recv1.at[s], device).start()
-
-        for k in range(1, slabs):
-            start({"gx": slab(k)})
-        for k in range(slabs):
-            start({"gx": slab(k), "gy": across})
-
-    def shared(s, sem):
-        window = obs_s.at[s, pl.ds(0, (2 * slabs - 1) * piece)]
-        pltpu.make_async_copy(window, window, sem.at[s]).wait()
-
-    def pass_on(s, i):
-        place = obs_s.at[s, band_rows((band, across)[i])]
-        return remote(place, place, send2.at[s, i], recv2.at[s, i], {"gy": partner})
-
-    def near_copy(t):
-        return remote(
-            table_ref.at[t], full_s.at[t, :, :, band_rows(band)], near_send.at[t], near_recv.at[t], {"gy": partner}
-        )
-
-    def far_copy(t):
-        return remote(
-            table_ref.at[t, :, near], full_s.at[t, :, near, band_rows(band)], far_send.at[t], far_recv.at[t],
-            {"gy": across},
-        )
-
-    def hand_copy(t):
-        place = full_s.at[t, :, far, band_rows(across)]
-        return remote(place, place, hand_send.at[t], hand_recv.at[t], {"gy": partner})
-
-    def send_table(t):
-        far_copy(t).start()
-        near_copy(t).start()
-
-    def hand_table(t):
-        far_copy(t).wait_recv()
-        hand_copy(t).start()
-
-    def own_tables():
-        return pltpu.make_async_copy(table_ref, full_s.at[:, :, :, band_rows(band)], own_sem)
-
-    def prepare(t, slot):
-        for k in range(2):
-            aside = full_s[t, k, far, half_rows(near), :]
-            blocks = (
-                (near, near, full_s[t, k, near, half_rows(near), :]),
-                (far, near, aside),
-                (near, far, aside.T),
-                (far, far, full_s[t, k, far, half_rows(far), :]),
-            )
-            for columns, rows, block in blocks:
-                here = pl.ds(pl.multiple_of(k * obs + rows * half, half), half)
-                high, low = split(block)
-                th_s[slot, columns, here, :] = high
-                tl_s[slot, columns, here, :] = low
-
-    barrier = pltpu.get_barrier_semaphore()
-    for k in range(1, slabs):
-        pl.semaphore_signal(barrier, inc=1, device_id={"gx": slab(k)}, device_id_type=MESH)
-    for k in range(slabs):
-        pl.semaphore_signal(barrier, inc=1, device_id={"gx": slab(k), "gy": across}, device_id_type=MESH)
-    pl.semaphore_signal(barrier, inc=1, device_id={"gy": partner}, device_id_type=MESH)
-    pl.semaphore_wait(barrier, 2 * slabs)
-
-    for p in range(2):
+    def spread_part(p):
         for k in range(1, slabs):
             reduce_copy(k, p).start()
-        if p == 0:
-            own_tables().start()
-            for t in range(first_tables):
-                send_table(t)
+
+    def stage(t, _):
+        b = order_ref[t]
+        for h in range(2):
+            full_s[t, 0, h, band_rows(band), :] = root_ref[b, :, h * half:(h + 1) * half]
+            full_s[t, 1, h, band_rows(band), :] = gain_ref[b, :, h * half:(h + 1) * half]
+        return 0
+
+    lax.fori_loop(ends[0], ends[1], pick, 0)
+    pl.semaphore_wait(barrier, 2 * slabs)
+    spread_part(0)
+    stage(0, 0)
+    send_table(0)
+    lax.fori_loop(ends[1], ends[2], pick, 0)
+    spread_part(1)
+    lax.fori_loop(1, batches, stage, 0)
+    lax.fori_loop(ends[2], ends[3], pick, 0)
 
     first_lat = lax.broadcasted_iota(jnp.int32, (1, obs), 1).astype(F32)
     first_lat = jnp.floor((first_lat + 0.5) * (1.0 / quarter)) * lat_dev
@@ -592,45 +593,59 @@
         z3_s[t] = jnp.zeros(z3_s.shape[1:], BF16)
     for s in range(batches, obs_s.shape[0]):
         obs_s[s] = jnp.zeros(obs_s.shape[1:], F32)
-    cells_s[...] = state_ref[...]
+    mine_s[...] = jnp.zeros_like(mine_s)
 
     def collect(p):
-        here = pl.ds(*parts[p])
-        total = packed_ref[column, here, :]
+        here = part_rows(p)
+        total = packed_s[column, here, :]
         for k in range(1, slabs):
             reduce_copy(k, p).wait_recv()
             total = total + land[k, here, :]
-        mine_s[here, :] = total
-
-    collect(0)
-    for s in range(early):
+        return total
+
+    mine_s[part_rows(0), :] = collect(0)
+    for s in range(ends[1]):
+        share_ranks(s)
+    mine_s[part_rows(1), :] = collect(1)
+    for s in range(ends[1], early):
         share(s)
-    for t in range(first_tables, ahead):
+    spread_part(2)
+    for s in range(ends[1]):
+        share_sides(s)
+    for t in range(1, ahead):
         send_table(t)
-    for t in range(min(3, batches)):
-        hand_table(t)
-    collect(1)
-    for s in range(early):
-        shared(s, recv1)
-        for i in range(2):
-            pass_on(s, i).start()
-    own_tables().wait()
+    hand_table(0)
     near_copy(0).wait_recv()
     hand_copy(0).wait_recv()
     prepare(0, 0)
-    for s in range(early):
+
+    def pass_both(s):
+        for i in range(2):
+            pass_on(s, i).start()
+
+    def passed(s):
         for i in range(2):
             pass_on(s, i).wait()
 
+    for s in range(2):
+        pieces(s, 3 * ranks, recv3)
+        pass_both(s)
+    for t in range(1, 3):
+        hand_table(t)
+    for s in range(2):
+        passed(s)
+    pieces(2, 3 * ranks, recv3)
+    for s in range(ends[1]):
+        pieces(s, 3 * ranks, send3)
+
     def state_wide(value):
-        high, low = split(value)
-        high, low = high.astype(F32), low.astype(F32)
+        low = value - value.astype(BF16).astype(F32)
         lane = lane_ids(value.shape)
         room = LANES - members
         moved = pltpu.roll(low, members, 1)
-        first = jnp.where(lane < members, high, moved)
-        last = jnp.where(lane < members - room, moved, pltpu.roll(high, members - room, 1))
-        return jnp.concatenate([first, last], axis=1).astype(BF16)
+        first = jnp.where(lane < members, value, moved)
+        last = jnp.where(lane < members - room, moved, pltpu.roll(value, members - room, 1))
+        return jnp.concatenate([first.astype(BF16), last.astype(BF16)], axis=1)
 
     def prior_tall(prior):
         high, low = split(prior.T[:members])
@@ -644,16 +659,16 @@
     def lat_weight(gap):
         return 1.0 - jnp.abs(gap)
 
-    def apply(rows, high, low, e):
-        both = nn(high, vw_s[e])
-        return rows - (both[:, :LANES] + both[:, LANES:] + nn(low, vw_s[e, :, :LANES]))
-
-    def gain_of(rows, taper, e):
-        return split(nn(state_wide(rows), z3_s[e]) * taper)
-
-    def update(rows, taper, e):
-        high, low = gain_of(rows, taper, e)
-        return apply(rows, high, low, e)
+    def apply(rows, high, low, vw):
+        both = nn(high, vw)
+        return rows - (both[:, :LANES] + both[:, LANES:] + nn(low, vw[:, :LANES]))
+
+    def gain_of(rows, taper, z3):
+        return split(nn(state_wide(rows), z3) * taper)
+
+    def update(rows, taper, z3, vw):
+        high, low = gain_of(rows, taper, z3)
+        return apply(rows, high, low, vw)
 
     def obs_taper(lat, bit, s, e):
         lon = (owner_ref[order_ref[jnp.minimum(s, batches - 1)]] * lon_dev).astype(F32)
@@ -661,42 +676,46 @@
         east = lon_weight(lon + 1.0 - lon_ref[e])
         return lat_weight(lat - lat_ref[e]) * (west + bit * (east - west))
 
-    def update_mine(e):
-        rows = mine_s[...]
+    def update_mine(rows, e, z3, vw):
         lat, lon = rows[:, members + 1:members + 2], rows[:, members + 2:members + 3]
         taper = lat_weight(lat - lat_ref[e]) * lon_weight(lon - lon_ref[e])
-        mine_s[...] = update(rows, taper, e)
-
-    def update_cells(e):
-        for i in range(classes // chunk):
-            tapers = []
-            for k in range(chunk):
-                c = i * chunk + k
-                lat = (band * lat_dev + c % lat_dev).astype(F32) * (1.0 / lat_total)
-                lon = (column * lon_dev + c // lat_dev).astype(F32)
-                weight = lat_weight(lat - lat_ref[e]) * lon_weight(lon - lon_ref[e])
-                tapers.append(jnp.broadcast_to(weight, (levels, obs)))
-            here = pl.ds(i * chunk * levels, chunk * levels)
-            cells_s[here, :] = update(cells_s[here, :], jnp.concatenate(tapers, axis=0), e)
-
-    def columns_of(rows):
-        return rows[:, members + 1:members + 2], rows[:, members + 4:members + 5]
+        return update(rows, taper, z3, vw)
+
+    def update_cells(e, part):
+        tapers = []
+        for k in range(chunk):
+            c = part * chunk + k
+            lat = (band * lat_dev + c % lat_dev).astype(F32) * (1.0 / lat_total)
+            lon = (column * lon_dev + c // lat_dev).astype(F32)
+            weight = lat_weight(lat - lat_ref[e]) * lon_weight(lon - lon_ref[e])
+            tapers.append(jnp.broadcast_to(weight, (levels, obs)))
+        here = pl.ds(part * chunk * levels, chunk * levels)
+        cells_s[here, :] = update(cells_s[here, :], jnp.concatenate(tapers, axis=0), z3_s[e], vw_s[e])
+
+    cell_parts = classes // chunk
 
     def turn(t, _):
         slot = lax.rem(t, 2)
         e = t + early
 
+        @pl.when(t == ends[2] - early)
+        def _():
+            rows = collect(2)
+            for k in range(ends[2] - early):
+                rows = update_mine(rows, early + k, z3_s[early + k], vw_s[early + k])
+            mine_s[part_rows(2), :] = rows
+
         @pl.when(e < batches)
         def _():
             share(e)
 
-        passing = e - 2
-
-        @pl.when(jnp.logical_and(passing >= early, passing < batches))
+        @pl.when(t + 2 < batches)
         def _():
-            shared(passing, recv1)
-            for i in range(2):
-                pass_on(passing, i).start()
+            pass_both(t + 2)
+
+        @pl.when(t + 3 < batches)
+        def _():
+            shared(t + 3, recv1)
 
         @pl.when(t + ahead < batches)
         def _():
@@ -711,15 +730,29 @@
             near_copy(t + 1).wait_recv()
             hand_copy(t + 1).wait_recv()
 
-        coming = t + 2
-
-        @pl.when(jnp.logical_and(coming >= early, coming < batches))
+        @pl.when(jnp.logical_and(t > 0, t + 1 < batches))
         def _():
-            for i in range(2):
-                pass_on(coming, i).wait()
-
-        prior = obs_s[t]
-        z3_s[e] = prior_tall(prior)
+            passed(t + 1)
+
+        prior = obs_s[t].reshape(obs, LANES)
+        rows = obs_s[t + 1].reshape(obs, LANES)
+        coming = t + 3
+        later = jnp.concatenate(
+            [obs_s[coming, place].reshape(quarter, LANES) for place in (band, across)], axis=0
+        )
+        lat, bit = rows[:, members + 1:members + 2], rows[:, members + 4:members + 5]
+        later_lat, later_bit = later[:, members + 1:members + 2], later[:, members + 4:members + 5]
+        done = 0
+
+        def some_cells(upto):
+            nonlocal done
+            while done < min(upto, cell_parts):
+                update_cells(e - 1, done)
+                done += 1
+
+        def catch_up(later, k, z3, vw):
+            return update(later, obs_taper(later_lat, later_bit, coming, e - k), z3, vw)
+
         lane = lane_ids(prior.shape)
         innovation = pltpu.roll(prior, LANES - 3, 1) - prior
         joined = jnp.where(lane < members, prior, jnp.where(lane == members, innovation, 0.0))
@@ -730,41 +763,50 @@
         part = both[:, :LANES] + both[:, LANES:] + nn(table_low, high)
         lane = lane_ids((obs, LANES))
         weighted = jnp.where(lane < members, part[:obs], jnp.where(lane == members, -part[obs:], 0.0))
-        vw_s[e] = jnp.concatenate(split(weighted * (1.0 / (members - 1.0))), axis=1)
-
-        rows = obs_s[t + 1]
-        lat, bit = columns_of(rows)
-        gained = gain_of(rows, obs_taper(lat, bit, t + 1, e), e)
-
-        update_cells(e - 1)
-
-        obs_s[t + 1] = apply(rows, *gained, e)
-        update_mine(e)
-
-        rows = obs_s[t + 2]
-        lat, bit = columns_of(rows)
-        for k in range(early - 2, -1, -1):
-            rows = update(rows, obs_taper(lat, bit, t + 2, e - k), e - k)
-        obs_s[t + 2] = rows
-
+        vw = jnp.concatenate(split(weighted * (1.0 / (members - 1.0))), axis=1)
+        z3 = prior_tall(prior)
+
+        later = catch_up(later, 2, z3_s[e - 2], vw_s[e - 2])
+        rows = update(rows, obs_taper(lat, bit, t + 1, e - 1), z3_s[e - 1], vw_s[e - 1])
+        some_cells(1)
+        gained = gain_of(rows, obs_taper(lat, bit, t + 1, e), z3)
+        later = catch_up(later, 1, z3_s[e - 1], vw_s[e - 1])
+        some_cells(2)
+        obs_s[t + 1] = apply(rows, *gained, vw).reshape(obs_s.shape[1:])
+        some_cells(3)
+        later = catch_up(later, 0, z3, vw)
+        for i, place in enumerate((band, across)):
+            obs_s[coming, place] = later[i * quarter:(i + 1) * quarter].reshape(obs_s.shape[2:])
+        mine_s[...] = update_mine(mine_s[...], e, z3, vw)
+        some_cells(cell_parts)
+        z3_s[e] = z3
+        vw_s[e] = vw
         prepare(jnp.minimum(t + 1, batches - 1), 1 - slot)
         return 0
 
     lax.fori_loop(0, batches, turn, 0)
-    update_cells(batches - 1 + early)
-
-    for p in range(2):
+    for i in range(cell_parts):
+        update_cells(batches - 1 + early, i)
+
+    for p in range(3):
         for k in range(1, slabs):
             reduce_copy(k, p).wait_send()
 
     def sent(t, _):
-        shared(t, send1)
         near_copy(t).wait_send()
         far_copy(t).wait_send()
         hand_copy(t).wait_send()
         return 0
 
     lax.fori_loop(0, batches, sent, 0)
+    for s in range(ends[1]):
+        pieces(s, ranks - 1, send1)
+
+    def shared_sent(s, _):
+        shared(s, send1)
+        return 0
+
+    lax.fori_loop(ends[1], batches, shared_sent, 0)
 
 
 def finish_kernel(cells_ref, anom_out, mean_out):
@@ -786,21 +828,6 @@
     piece = quarter // slabs
     early = min(EARLY, batches)
     lat_total = float(bands * lat_dev)
-    state, packed, table = pl.pallas_call(
-        functools.partial(arrange_kernel, lon_dev, lat_dev, lat_total),
-        out_shape=(
-            jax.ShapeDtypeStruct((cells, LANES), F32),
-            jax.ShapeDtypeStruct((slabs, batches * piece, LANES), F32),
-            jax.ShapeDtypeStruct((batches, 2, 2, quarter, half), F32),
-        ),
-        in_specs=[SMEM] * 4 + [VMEM] * 4,
-        out_specs=(VMEM, VMEM, VMEM),
-        name="arrange",
-    )(
-        obs_cell, obs_value, owner, order,
-        anomalies.reshape(members, classes, levels), state_mean.reshape(classes, levels), root_inv, gain_inv,
-    )
-
     sizes = (
         members, lon_dev, lat_dev, levels, float(slabs * lon_dev), lat_total, REACH * lon_dev + 1.0, bands, slabs, early
     )
@@ -808,31 +835,36 @@
     cells_out = pl.pallas_call(
         functools.partial(analysis_kernel, sizes),
         out_shape=jax.ShapeDtypeStruct((cells, LANES), F32),
-        in_specs=[SMEM] * 2 + [VMEM] * 4,
+        in_specs=[SMEM] * 3 + [VMEM] * 6,
         out_specs=VMEM,
         scratch_shapes=[
             pltpu.VMEM((batches + early, 1, obs), F32),
             pltpu.VMEM((batches + early, 1, obs), F32),
+            pltpu.VMEM((quarter, LANES), F32),
+            pltpu.VMEM((slabs, batches * piece, LANES), F32),
             pltpu.VMEM((slabs, batches * piece, LANES), F32),
             pltpu.VMEM((batches * piece, LANES), F32),
             pltpu.VMEM((batches, piece, LANES), F32),
-            pltpu.VMEM((batches + 2, obs, LANES), F32),
+            pltpu.VMEM((batches + 3, bands, slabs // 2, 2, piece, LANES), F32),
             pltpu.VMEM((batches, 2, 2, obs, half), F32),
             pltpu.VMEM((2, 2, 2 * obs, half), BF16),
             pltpu.VMEM((2, 2, 2 * obs, half), BF16),
             pltpu.VMEM((batches + early, 2 * LANES, obs), BF16),
             pltpu.VMEM((batches + early, obs, 2 * LANES), BF16),
-            dma((2, slabs)), dma((2, slabs)),
+            dma((3, slabs)), dma((3, slabs)),
             dma((batches,)), dma((batches,)),
             dma((batches, 2)), dma((batches, 2)),
+            dma((3,)), dma((3,)),
             dma((batches,)), dma((batches,)),
             dma((batches,)), dma((batches,)),
             dma((batches,)), dma((batches,)),
-            dma,
         ],
         compiler_params=pltpu.CompilerParams(collective_id=0, has_side_effects=True),
         name="analysis",
-    )(order, owner, state, packed, table, obs_cell)
+    )(
+        obs_cell, order, owner, obs_cell, obs_value,
+        anomalies.reshape(members, classes, levels), state_mean.reshape(classes, levels), root_inv, gain_inv,
+    )
 
     post, mean = pl.pallas_call(
         finish_kernel,

time: 92.7 us -> 73.9 us (0.80)
  Pallas kernels: 91.9 us -> 73.1 us
    pallas_call x1, Pallas kernels: 83.9 us -> 70.6 us  [near_local(): pl.pallas_call(functools.partial(analysis_kernel, sizes), out_shape=jax.S...]
    pallas_call x1 -> x0, Pallas kernels: 5.44 us -> none  [near_local(): pl.pallas_call(functools.partial(arrange_kernel, lon_dev, lat_dev, lat_to...]
where the time goes in v2:
time: 73.9 us; the launch traced here: 73.7 us
  Pallas kernels  73.1 us (99%)
    pallas_call x1, Pallas kernels, near_local(): pl.pallas_call(functools.partial(analysis_kernel, sizes), out_shape=jax.S...  70.6 us
    pallas_call x1, Pallas kernels, near_local(): pl.pallas_call(finish_kernel, out_shape=(jax.ShapeDtypeStruct((members, c...  2.51 us

profile of v2, /device:TPU:0, one launch (start us, length us, event | category | flops | bytes accessed | tf_op | source)
XLA Modules:
  0.0 73.7 jit_solution(7634981161873374522)
XLA Ops:
  0.6 70.6 %analysis.1.cells_ref = f32[2048,128]{1,0:T(8,128)} custom-call(s32[16,256]{1,0:T(8,128)} %cell_ref.1, s32[16]{0:T(128)} %order_ref.1, s32[16]{0:T(128)} %owner_ref.1, s32[16,256]{1,0:T(8,128)} %cell_ref.1, f32[16,64]{1,0:T(8,128)} %value_ref.1, f32[80,16,128]{2,1,0:T(8,128)} %bitcast.4, f32[16,128]{1,0:T(8,128)} %bitcast.5, f32[16,64,256]{2,1,0:T(8,128)} %root_ref.1, ...), custom_call_target="tpu_custom_call" | custom-call | tf_op jit(solution)/shard_map/analysis/pallas_call | solution.py:835
  71.2 2.5 %finish.1 = (f32[80,16,128]{2,1,0:T(8,128)}, f32[16,128]{1,0:T(8,128)}) custom-call(f32[2048,128]{1,0:T(8,128)} %analysis.1.cells_ref), custom_call_target="tpu_custom_call" | custom-call | tf_op jit(solution)/shard_map/finish/pallas_call | solution.py:869

commit v3 on v2

--- a/solution.py
+++ b/solution.py
@@ -404,14 +404,14 @@
     batches, obs = cell_ref.shape
     quarter, half = obs // bands, obs // 2
     piece = quarter // slabs
-    ahead = min(5, batches)
+    ahead, prompt = min(6, batches), min(4, batches)
     column, band = lax.axis_index("gx"), lax.axis_index("gy")
     partner = band + 1 - 2 * lax.rem(band, 2)
     across = lax.rem(band + bands // 2, bands)
     near = lax.div(band, bands // 2)
     far = 1 - near
     classes = lon_dev * lat_dev
-    chunk = 4
+    chunk = 8
 
     def slab(k):
         return lax.rem(column + k, slabs)
@@ -576,6 +576,8 @@
     lax.fori_loop(ends[1], ends[2], pick, 0)
     spread_part(1)
     lax.fori_loop(1, batches, stage, 0)
+    for t in range(1, prompt):
+        send_table(t)
     lax.fori_loop(ends[2], ends[3], pick, 0)
 
     first_lat = lax.broadcasted_iota(jnp.int32, (1, obs), 1).astype(F32)
@@ -612,7 +614,7 @@
     spread_part(2)
     for s in range(ends[1]):
         share_sides(s)
-    for t in range(1, ahead):
+    for t in range(prompt, ahead):
         send_table(t)
     hand_table(0)
     near_copy(0).wait_recv()
@@ -660,8 +662,12 @@
         return 1.0 - jnp.abs(gap)
 
     def apply(rows, high, low, vw):
-        both = nn(high, vw)
-        return rows - (both[:, :LANES] + both[:, LANES:] + nn(low, vw[:, :LANES]))
+        both = nn(jnp.concatenate([high, low], axis=1), vw)
+        return rows - (both[:, :LANES] + both[:, LANES:])
+
+    def tall(high, low):
+        under = jnp.concatenate([high, jnp.zeros_like(high)], axis=1)
+        return jnp.concatenate([jnp.concatenate([high, low], axis=1), under], axis=0)
 
     def gain_of(rows, taper, z3):
         return split(nn(state_wide(rows), z3) * taper)
@@ -676,10 +682,12 @@
         east = lon_weight(lon + 1.0 - lon_ref[e])
         return lat_weight(lat - lat_ref[e]) * (west + bit * (east - west))
 
+    def mine_taper(rows, e):
+        lat, lon = rows[:, members + 1:members + 2], rows[:, members + 2:members + 3]
+        return lat_weight(lat - lat_ref[e]) * lon_weight(lon - lon_ref[e])
+
     def update_mine(rows, e, z3, vw):
-        lat, lon = rows[:, members + 1:members + 2], rows[:, members + 2:members + 3]
-        taper = lat_weight(lat - lat_ref[e]) * lon_weight(lon - lon_ref[e])
-        return update(rows, taper, z3, vw)
+        return update(rows, mine_taper(rows, e), z3, vw)
 
     def update_cells(e, part):
         tapers = []
@@ -759,26 +767,26 @@
         high, low = split(joined)
         table_high = jnp.concatenate([th_s[slot, 0], th_s[slot, 1]], axis=1)
         table_low = jnp.concatenate([tl_s[slot, 0], tl_s[slot, 1]], axis=1)
-        both = nn(table_high, jnp.concatenate([high, low], axis=1))
-        part = both[:, :LANES] + both[:, LANES:] + nn(table_low, high)
+        both = nn(jnp.concatenate([table_high, table_low], axis=1), tall(high, low))
+        part = both[:, :LANES] + both[:, LANES:]
         lane = lane_ids((obs, LANES))
         weighted = jnp.where(lane < members, part[:obs], jnp.where(lane == members, -part[obs:], 0.0))
-        vw = jnp.concatenate(split(weighted * (1.0 / (members - 1.0))), axis=1)
+        vw = tall(*split(weighted * (1.0 / (members - 1.0))))
         z3 = prior_tall(prior)
 
         later = catch_up(later, 2, z3_s[e - 2], vw_s[e - 2])
-        rows = update(rows, obs_taper(lat, bit, t + 1, e - 1), z3_s[e - 1], vw_s[e - 1])
-        some_cells(1)
-        gained = gain_of(rows, obs_taper(lat, bit, t + 1, e), z3)
-        later = catch_up(later, 1, z3_s[e - 1], vw_s[e - 1])
-        some_cells(2)
-        obs_s[t + 1] = apply(rows, *gained, vw).reshape(obs_s.shape[1:])
-        some_cells(3)
-        later = catch_up(later, 0, z3, vw)
+        tapers = (obs_taper(lat, bit, t + 1, e - 1), obs_taper(later_lat, later_bit, coming, e - 1))
+        both = update(jnp.concatenate([rows, later], axis=0), jnp.concatenate(tapers, axis=0), z3_s[e - 1], vw_s[e - 1])
+        rows, later = both[:obs], both[obs:]
+        some_cells(cell_parts)
+        mine = mine_s[...]
+        joint = jnp.concatenate([rows, later, mine], axis=0)
+        tapers = (obs_taper(lat, bit, t + 1, e), obs_taper(later_lat, later_bit, coming, e), mine_taper(mine, e))
+        joint = update(joint, jnp.concatenate(tapers, axis=0), z3, vw)
+        obs_s[t + 1] = joint[:obs].reshape(obs_s.shape[1:])
         for i, place in enumerate((band, across)):
-            obs_s[coming, place] = later[i * quarter:(i + 1) * quarter].reshape(obs_s.shape[2:])
-        mine_s[...] = update_mine(mine_s[...], e, z3, vw)
-        some_cells(cell_parts)
+            obs_s[coming, place] = joint[obs + i * quarter:obs + (i + 1) * quarter].reshape(obs_s.shape[2:])
+        mine_s[...] = joint[obs + 2 * quarter:]
         z3_s[e] = z3
         vw_s[e] = vw
         prepare(jnp.minimum(t + 1, batches - 1), 1 - slot)
@@ -850,7 +858,7 @@
             pltpu.VMEM((2, 2, 2 * obs, half), BF16),
             pltpu.VMEM((2, 2, 2 * obs, half), BF16),
             pltpu.VMEM((batches + early, 2 * LANES, obs), BF16),
-            pltpu.VMEM((batches + early, obs, 2 * LANES), BF16),
+            pltpu.VMEM((batches + early, 2 * obs, 2 * LANES), BF16),
             dma((3, slabs)), dma((3, slabs)),
             dma((batches,)), dma((batches,)),
             dma((batches, 2)), dma((batches, 2)),

time: 73.9 us -> 67.2 us (0.909)
  Pallas kernels: 73.1 us -> 66.4 us
    pallas_call x1, Pallas kernels: 70.6 us -> 63.8 us  [near_local(): pl.pallas_call(functools.partial(analysis_kernel, sizes), out_shape=jax.S...]
where the time goes in v3:
time: 67.2 us; the launch traced here: 67 us
  Pallas kernels  66.4 us (99%)
    pallas_call x1, Pallas kernels, near_local(): pl.pallas_call(functools.partial(analysis_kernel, sizes), out_shape=jax.S...  63.8 us
    pallas_call x1, Pallas kernels, near_local(): pl.pallas_call(finish_kernel, out_shape=(jax.ShapeDtypeStruct((members, c...  2.51 us

profile of v3, /device:TPU:0, one launch (start us, length us, event | category | flops | bytes accessed | tf_op | source)
XLA Modules:
  0.0 67.0 jit_solution(12084046394442727774)
XLA Ops:
  0.6 63.8 %analysis.1.cells_ref = f32[2048,128]{1,0:T(8,128)} custom-call(s32[16,256]{1,0:T(8,128)} %cell_ref.1, s32[16]{0:T(128)} %order_ref.1, s32[16]{0:T(128)} %owner_ref.1, s32[16,256]{1,0:T(8,128)} %cell_ref.1, f32[16,64]{1,0:T(8,128)} %value_ref.1, f32[80,16,128]{2,1,0:T(8,128)} %bitcast.4, f32[16,128]{1,0:T(8,128)} %bitcast.5, f32[16,64,256]{2,1,0:T(8,128)} %root_ref.1, ...), custom_call_target="tpu_custom_call" | custom-call | tf_op jit(solution)/shard_map/analysis/pallas_call | solution.py:843
  64.5 2.5 %finish.1 = (f32[80,16,128]{2,1,0:T(8,128)}, f32[16,128]{1,0:T(8,128)}) custom-call(f32[2048,128]{1,0:T(8,128)} %analysis.1.cells_ref), custom_call_target="tpu_custom_call" | custom-call | tf_op jit(solution)/shard_map/finish/pallas_call | solution.py:877

commit v4 on v3

--- a/solution.py
+++ b/solution.py
@@ -404,7 +404,7 @@
     batches, obs = cell_ref.shape
     quarter, half = obs // bands, obs // 2
     piece = quarter // slabs
-    ahead, prompt = min(6, batches), min(4, batches)
+    ahead, prompt = min(8, batches), min(6, batches)
     column, band = lax.axis_index("gx"), lax.axis_index("gy")
     partner = band + 1 - 2 * lax.rem(band, 2)
     across = lax.rem(band + bands // 2, bands)
@@ -467,11 +467,10 @@
 
     def share(s):
         start = keep(s)
-
+        for k in range(slabs // 2, slabs + slabs // 2):
+            start({"gx": slab(k % slabs), "gy": across})
         for k in range(1, slabs):
-            start({"gx": slab(k)})
-        for k in range(slabs):
-            start({"gx": slab(k), "gy": across})
+            start({"gx": slab((k + slabs // 2 - 1) % (slabs - 1) + 1)})
 
     def pieces(s, count, sem):
         window = mine_s.at[pl.ds(0, count * piece)]

time: 67.2 us -> 66.3 us (0.987)
  Pallas kernels: 66.4 us -> 65.5 us
    pallas_call x1, Pallas kernels: 63.8 us -> 63 us  [near_local(): pl.pallas_call(functools.partial(analysis_kernel, sizes), out_shape=jax.S...]
where the time goes in v4:
time: 66.3 us; the launch traced here: 66.2 us
  Pallas kernels  65.5 us (99%)
    pallas_call x1, Pallas kernels, near_local(): pl.pallas_call(functools.partial(analysis_kernel, sizes), out_shape=jax.S...  63 us
    pallas_call x1, Pallas kernels, near_local(): pl.pallas_call(finish_kernel, out_shape=(jax.ShapeDtypeStruct((members, c...  2.51 us

profile of v4, /device:TPU:0, one launch (start us, length us, event | category | flops | bytes accessed | tf_op | source)
XLA Modules:
  0.0 66.2 jit_solution(16164031262133940463)
XLA Ops:
  0.6 63.0 %analysis.1.cells_ref = f32[2048,128]{1,0:T(8,128)} custom-call(s32[16,256]{1,0:T(8,128)} %cell_ref.1, s32[16]{0:T(128)} %order_ref.1, s32[16]{0:T(128)} %owner_ref.1, s32[16,256]{1,0:T(8,128)} %cell_ref.1, f32[16,64]{1,0:T(8,128)} %value_ref.1, f32[80,16,128]{2,1,0:T(8,128)} %bitcast.4, f32[16,128]{1,0:T(8,128)} %bitcast.5, f32[16,64,256]{2,1,0:T(8,128)} %root_ref.1, ...), custom_call_target="tpu_custom_call" | custom-call | tf_op jit(solution)/shard_map/analysis/pallas_call | solution.py:842
  63.6 2.5 %finish.1 = (f32[80,16,128]{2,1,0:T(8,128)}, f32[16,128]{1,0:T(8,128)}) custom-call(f32[2048,128]{1,0:T(8,128)} %analysis.1.cells_ref), custom_call_target="tpu_custom_call" | custom-call | tf_op jit(solution)/shard_map/finish/pallas_call | solution.py:876

commit v5 on v4

--- a/solution.py
+++ b/solution.py
@@ -485,18 +485,18 @@
 
     def near_copy(t):
         return remote(
-            full_s.at[t, :, :, band_rows(band)], full_s.at[t, :, :, band_rows(band)], near_send.at[t], near_recv.at[t], {"gy": partner}
+            full_s.at[t, :, :, band_rows(band)], full_s.at[t, :, :, band_rows(band)], near_send, near_recv.at[t], {"gy": partner}
         )
 
     def far_copy(t):
         return remote(
-            full_s.at[t, :, near, band_rows(band)], full_s.at[t, :, near, band_rows(band)], far_send.at[t],
+            full_s.at[t, :, near, band_rows(band)], full_s.at[t, :, near, band_rows(band)], far_send,
             far_recv.at[t], {"gy": across},
         )
 
     def hand_copy(t):
         place = full_s.at[t, :, far, band_rows(across)]
-        return remote(place, place, hand_send.at[t], hand_recv.at[t], {"gy": partner})
+        return remote(place, place, hand_send, hand_recv.at[t], {"gy": partner})
 
     def send_table(t):
         far_copy(t).start()
@@ -799,13 +799,12 @@
         for k in range(1, slabs):
             reduce_copy(k, p).wait_send()
 
-    def sent(t, _):
-        near_copy(t).wait_send()
-        far_copy(t).wait_send()
-        hand_copy(t).wait_send()
-        return 0
-
-    lax.fori_loop(0, batches, sent, 0)
+    for window, sem in (
+        (full_s.at[:, :, :, band_rows(band)], near_send),
+        (full_s.at[:, :, near, band_rows(band)], far_send),
+        (full_s.at[:, :, far, band_rows(across)], hand_send),
+    ):
+        pltpu.make_async_copy(window, window, sem).wait()
     for s in range(ends[1]):
         pieces(s, ranks - 1, send1)
 
@@ -862,9 +861,9 @@
             dma((batches,)), dma((batches,)),
             dma((batches, 2)), dma((batches, 2)),
             dma((3,)), dma((3,)),
-            dma((batches,)), dma((batches,)),
-            dma((batches,)), dma((batches,)),
-            dma((batches,)), dma((batches,)),
+            dma, dma((batches,)),
+            dma, dma((batches,)),
+            dma, dma((batches,)),
         ],
         compiler_params=pltpu.CompilerParams(collective_id=0, has_side_effects=True),
         name="analysis",

time: 66.3 us -> 65.8 us (level)
  no operation moved by 1% of the time
where the time goes in v5:
time: 65.8 us; the launch traced here: 65.6 us
  Pallas kernels  65 us (99%)
    pallas_call x1, Pallas kernels, near_local(): pl.pallas_call(functools.partial(analysis_kernel, sizes), out_shape=jax.S...  62.5 us
    pallas_call x1, Pallas kernels, near_local(): pl.pallas_call(finish_kernel, out_shape=(jax.ShapeDtypeStruct((members, c...  2.51 us

profile of v5, /device:TPU:0, one launch (start us, length us, event | category | flops | bytes accessed | tf_op | source)
XLA Modules:
  0.0 65.6 jit_solution(16644712513604443812)
XLA Ops:
  0.6 62.5 %analysis.1.cells_ref = f32[2048,128]{1,0:T(8,128)} custom-call(s32[16,256]{1,0:T(8,128)} %cell_ref.1, s32[16]{0:T(128)} %order_ref.1, s32[16]{0:T(128)} %owner_ref.1, s32[16,256]{1,0:T(8,128)} %cell_ref.1, f32[16,64]{1,0:T(8,128)} %value_ref.1, f32[80,16,128]{2,1,0:T(8,128)} %bitcast.4, f32[16,128]{1,0:T(8,128)} %bitcast.5, f32[16,64,256]{2,1,0:T(8,128)} %root_ref.1, ...), custom_call_target="tpu_custom_call" | custom-call | tf_op jit(solution)/shard_map/analysis/pallas_call | solution.py:841
  63.1 2.5 %finish.1 = (f32[80,16,128]{2,1,0:T(8,128)}, f32[16,128]{1,0:T(8,128)}) custom-call(f32[2048,128]{1,0:T(8,128)} %analysis.1.cells_ref), custom_call_target="tpu_custom_call" | custom-call | tf_op jit(solution)/shard_map/finish/pallas_call | solution.py:875
